TPU v7x, 32 devices: a whole 2x2x4 slice. The times are simulated.
32 devices in a mesh: ga: 8 (over z, x), band: 4 (over y, core).
Axes of the slice: x: 2, y: 2, z: 4, core: 2. Of those that a mesh axis runs over, the one named last changes fastest.
Arguments:
- waves: float32 [2, 8192, 1024], P(None, 'ga', 'band'), may hold values from -6 to 6
- miller: int32 [3, 8192], P(None, 'ga'), may hold values from -8 to 8
- positions: float32 [64, 3], replicated, may hold values from 0 to 1
- form_factors: float32 [4, 18, 8192], P(None, None, 'ga'), may hold values from -0.0625 to 0.0625
- coupling: float32 [4, 18, 18], replicated, may hold values from -1.6970563 to 5.656854
- species: int32 [64], replicated, may hold values from 0 to 3
- block_sizes: int32 [64], replicated, may hold values from 1 to 18, 512 in all
- occupation: float32 [1024], P('band'), may hold values from 0.05 to 2
Outputs:
- residual: float32 [2, 8192, 1024], P(None, 'ga', 'band')
- estimate: float32 [1024], P('band')
- energy: float32 [], replicated
All inputs are finite; a program needn't handle non-finite values.
Results may differ from a plain program's by a relative error of at most 0.00007.
Values sent between devices are 32-bit elements; how exact they have to be, the bound alone decides.
A program may use at most 64 MiB of HBM per device.

v0:
```python
import jax
import jax.numpy as jnp
from jax import lax
from jax.sharding import PartitionSpec as P

PROJ = 512


TWO_PI = 6.283185307179586
KINETIC_SCALE = 0.005
EPSILON = 1e-06
HIGHEST_PRECISION = lax.Precision.HIGHEST


def tables(miller, positions, form_factors, coupling, species, block_sizes):
    nspec, kmax, local_waves = form_factors.shape
    atoms = block_sizes.shape[0]
    block_ends = jnp.cumsum(block_sizes)
    block_starts = block_ends - block_sizes
    columns = lax.iota(jnp.int32, PROJ)
    owner_atom = jnp.sum((block_ends[None, :] <= columns[:, None]).astype(jnp.int32), axis=1)
    owner_match = owner_atom[:, None] == lax.iota(jnp.int32, atoms)[None, :]
    owner_hot = owner_match.astype(jnp.float32)
    channel = columns - jnp.sum(jnp.where(owner_match, block_starts[None, :], 0), axis=1)
    species_of = jnp.sum(jnp.where(owner_match, species[None, :], 0), axis=1)
    row_index = species_of * kmax + channel
    row_hot = (row_index[:, None] == lax.iota(jnp.int32, nspec * kmax)[None, :]).astype(jnp.float32)
    radial = jnp.dot(
        row_hot, form_factors.reshape(nspec * kmax, local_waves), precision=HIGHEST_PRECISION
    )
    miller_f = miller.astype(jnp.float32)
    phases = TWO_PI * (
        positions[:, 0:1] * miller_f[0][None, :]
        + positions[:, 1:2] * miller_f[1][None, :]
        + positions[:, 2:3] * miller_f[2][None, :]
    )
    cosine_rows = jnp.dot(owner_hot, jnp.cos(phases), precision=HIGHEST_PRECISION)
    sine_rows = jnp.dot(owner_hot, jnp.sin(phases), precision=HIGHEST_PRECISION)
    beta_re = radial * cosine_rows
    beta_im = -(radial * sine_rows)
    coupling_rows = jnp.dot(
        row_hot, coupling.reshape(nspec * kmax, kmax), precision=HIGHEST_PRECISION
    )
    channel_hot = (channel[:, None] == lax.iota(jnp.int32, kmax)[None, :]).astype(jnp.float32)
    dense = jnp.dot(coupling_rows, channel_hot.T, precision=HIGHEST_PRECISION)
    dense = jnp.where(owner_atom[:, None] == owner_atom[None, :], dense, jnp.zeros_like(dense))
    kinetic = (
        0.5
        * KINETIC_SCALE
        * (miller_f[0] * miller_f[0] + miller_f[1] * miller_f[1] + miller_f[2] * miller_f[2])
    )
    return (beta_re, beta_im, dense, kinetic)


def apply_blocks(dense, projection):
    return jnp.stack(
        [
            jnp.dot(dense, projection[0], precision=HIGHEST_PRECISION),
            jnp.dot(dense, projection[1], precision=HIGHEST_PRECISION),
        ]
    )


def quotients(projection, mixed_proj, kin_sum, norm_sum):
    nonlocal_sum = jnp.sum(projection[0] * mixed_proj[0] + projection[1] * mixed_proj[1], axis=0)
    estimate = (kin_sum + nonlocal_sum) / (norm_sum + EPSILON)
    nonlocal_share = nonlocal_sum / (norm_sum + EPSILON)
    return (estimate, nonlocal_share)


def on_device(waves, miller, positions, form_factors, coupling, species, block_sizes, occupation):
    beta_re, beta_im, dense, kinetic = tables(
        miller, positions, form_factors, coupling, species, block_sizes
    )
    psi_re = waves[0]
    psi_im = waves[1]
    proj_re = jnp.dot(beta_re, psi_re, precision=HIGHEST_PRECISION) + jnp.dot(
        beta_im, psi_im, precision=HIGHEST_PRECISION
    )
    proj_im = jnp.dot(beta_re, psi_im, precision=HIGHEST_PRECISION) - jnp.dot(
        beta_im, psi_re, precision=HIGHEST_PRECISION
    )
    proj_part = jnp.stack([proj_re, proj_im])
    density = psi_re * psi_re + psi_im * psi_im
    kin_part = jnp.sum(kinetic[:, None] * density, axis=0)
    norm_part = jnp.sum(density, axis=0)
    summed = lax.psum((proj_part, kin_part, norm_part), "ga")
    projection, kin_sum, norm_sum = summed
    mixed_proj = apply_blocks(dense, projection)
    estimate, nonlocal_share = quotients(projection, mixed_proj, kin_sum, norm_sum)
    contract = (((0,), (0,)), ((), ()))
    applied_re = lax.dot_general(
        beta_re, mixed_proj[0], contract, precision=HIGHEST_PRECISION
    ) - lax.dot_general(beta_im, mixed_proj[1], contract, precision=HIGHEST_PRECISION)
    applied_im = lax.dot_general(
        beta_re, mixed_proj[1], contract, precision=HIGHEST_PRECISION
    ) + lax.dot_general(beta_im, mixed_proj[0], contract, precision=HIGHEST_PRECISION)
    shifted = kinetic[:, None] - estimate[None, :]
    residual = jnp.stack([shifted * psi_re + applied_re, shifted * psi_im + applied_im])
    energy = lax.psum(jnp.sum(occupation * nonlocal_share), "band")
    return (residual, estimate, energy)


def solution(mesh):
    in_specs = (
        P(None, "ga", "band"),
        P(None, "ga"),
        P(),
        P(None, None, "ga"),
        P(),
        P(),
        P(),
        P("band"),
    )
    out_specs = (P(None, "ga", "band"), P("band"), P())
    return jax.shard_map(
        on_device, mesh=mesh, in_specs=in_specs, out_specs=out_specs, check_vma=False
    )
```

profile of v0, /device:TPU:0, one launch (start us, length us, event | category | flops | bytes accessed | tf_op | source)
XLA Modules:
  0.0 145.8 jit_solution(10682692655610408835)
XLA Ops:
  7.2 0.0 all-reduce.3.cloned.1.call-start
  7.2 0.7 copy.15
  8.0 0.1 reduce-window.8
  8.1 0.1 reduce
  8.2 0.7 sub.33
  8.8 0.1 convert_reduce_fusion
  8.9 0.8 slice_bitcast_fusion.6
  9.7 0.7 convert_element_type.4
  10.5 1.1 copy.16
  11.6 0.8 select_reduce_fusion
  12.4 1.0 fusion.22
  13.4 2.0 %multiply_negate_fusion = f32[512,1024]{1,0:T(8,128)S(1)} fusion(f32[512,1024]{1,0:T(8,128)S(1)} %fusion.22, f32[1024]{0:T(1024)S(1)} %bitcast.78, f32[64]{0:T(128)S(1)} %get-tuple-element.17, f32[1024]{0:T(1024)S(1)} %bitcast.81, f32[64]{0:T(128)S(1)} %get-tuple-element.18, f32[1024]{0:T(1024)S(1)} %bitcast.75, f32[64]{0:T(128)S(1)} %get-tuple-element.16, ...), kind=kOutput, calls=%fused_computation.1 | convolution fusion | flops 404127744 | bytes 4209408 | tf_op jit(solution)/shard_map/dot_general | solution.py:38
  15.5 0.0 copy-start
  15.5 0.0 copy-start.2
  15.5 2.0 %convolution_multiply_fusion = f32[512,1024]{1,0:T(8,128)S(1)} fusion(f32[512,1024]{1,0:T(8,128)S(1)} %fusion.22, f32[1024]{0:T(1024)S(1)} %bitcast.79, f32[64]{0:T(128)S(1)} %get-tuple-element.17, f32[1024]{0:T(1024)S(1)} %bitcast.82, f32[64]{0:T(128)S(1)} %get-tuple-element.18, f32[1024]{0:T(1024)S(1)} %bitcast.76, f32[64]{0:T(128)S(1)} %get-tuple-element.16, ...), kind=kOutput, calls=%fused_computation.2 | convolution fusion | flops 403603456 | bytes 4209408 | tf_op jit(solution)/shard_map/dot_general | solution.py:37
  17.5 0.4 copy-done.2
  17.8 1.8 %fusion.6 = f32[512,256]{1,0:T(8,128)S(1)} fusion(f32[512,1024]{1,0:T(8,128)S(1)} %convolution_multiply_fusion, f32[2,1024,256]{2,1,0:T(8,128)S(1)} %copy-done.2), kind=kOutput, calls=%fused_computation.17 | convolution fusion | flops 1610612736 | bytes 3670016 | tf_op jit(solution)/shard_map/dot_general | solution.py:80
  19.7 1.8 %fusion.11 = f32[512,256]{1,0:T(8,128)S(1)} fusion(f32[512,1024]{1,0:T(8,128)S(1)} %convolution_multiply_fusion, f32[2,1024,256]{2,1,0:T(8,128)S(1)} %copy-done.2), kind=kOutput, calls=%fused_computation.23 | convolution fusion | flops 1610612736 | bytes 3670016 | tf_op jit(solution)/shard_map/dot_general | solution.py:77
  21.5 1.8 %fusion.4 = f32[1,512,256]{2,1,0:T(8,128)S(1)} fusion(f32[512,256]{1,0:T(8,128)S(1)} %fusion.6, f32[512,1024]{1,0:T(8,128)S(1)} %multiply_negate_fusion, f32[2,1024,256]{2,1,0:T(8,128)S(1)} %copy-done.2), kind=kOutput, calls=%fused_computation.13 | convolution fusion | flops 1610743808 | bytes 4194304 | tf_op jit(solution)/shard_map/dot_general | solution.py:80
  23.3 2.0 %fusion.5 = f32[1,512,256]{2,1,0:T(8,128)S(1)} fusion(f32[512,256]{1,0:T(8,128)S(1)} %fusion.11, f32[512,1024]{1,0:T(8,128)S(1)} %multiply_negate_fusion, f32[2,1024,256]{2,1,0:T(8,128)S(1)} %copy-done.2), kind=kOutput, calls=%fused_computation.15 | convolution fusion | flops 1610743808 | bytes 4194304 | tf_op jit(solution)/shard_map/dot_general | solution.py:77
  25.3 0.0 copy-start.9
  25.3 1.1 pad_maximum_fusion.1
  26.4 0.0 all-reduce.3.cloned.1.call-update
  26.4 0.1 copy.17
  26.5 0.1 reshape.75
  26.6 1.8 %fusion.23 = (f32[256]{0:T(256)S(1)}, f32[256]{0:T(256)S(1)}) fusion(f32[2,1024,256]{2,1,0:T(8,128)} %param.8, f32[1024]{0:T(1024)S(1)} %add_multiply_fusion.3), kind=kLoop, calls=%fused_computation.43 | loop fusion | flops 1572352 | bytes 2103296 | tf_op jit(solution)/shard_map/reduce_sum | solution.py:86
  28.4 23.6 %all-reduce = (f32[256]{0:T(256)S(1)}, f32[256]{0:T(256)S(1)}) all-reduce(f32[256]{0:T(256)S(1)} %get-tuple-element.4, f32[256]{0:T(256)S(1)} %get-tuple-element.3), channel_id=1, replica_groups=mesh['ga'=8,'band'=4] {'ga'}, use_global_device_ids=true, to_apply=%region_1.2 | all-reduce | flops 512 | bytes 4096 | tf_op jit(solution)/shard_map/psum | solution.py:87
  52.0 0.3 fusion.21
  52.3 0.7 convolution_select_fusion
  53.1 54.6 %all-reduce.3.cloned.1.call-done = f32[2,512,256]{2,1,0:T(8,128)} async-done(((f32[2,512,256]{2,1,0:T(8,128)}), f32[2,512,256]{2,1,0:T(8,128)}) %all-reduce.3.cloned.1.call-update) | async-done | bytes 1048592 | tf_op jit(solution)/shard_map/psum | solution.py:87
  107.7 2.0 %fusion.17 = f32[512,256]{1,0:T(8,128)S(1)} fusion(f32[512,512]{1,0:T(8,128)S(1)} %convolution_select_fusion, f32[2,512,256]{2,1,0:T(8,128)} %all-reduce.3.cloned.1.call-done), kind=kOutput, calls=%fused_computation.34 | convolution fusion | flops 805306368 | bytes 2097152 | tf_op jit(solution)/shard_map/dot_general | solution.py:58
  109.7 4.4 %fusion.46 = f32[1024,256]{1,0:T(8,128)} fusion(f32[512,1024]{1,0:T(8,128)S(1)} %convolution_multiply_fusion, f32[512,256]{1,0:T(8,128)S(1)} %fusion.17), kind=kOutput, calls=%fused_computation.79 | convolution fusion | flops 1610612736 | bytes 3670016 | tf_op jit(solution)/shard_map/dot_general | solution.py:92
  114.2 0.0 copy-done.8
  114.2 1.8 %add_reduce_fusion = (f32[256]{0:T(256)S(1)}, f32[512,256]{1,0:T(8,128)}) fusion(f32[512,256]{1,0:T(8,128)S(1)} %fusion.17, f32[2,512,256]{2,1,0:T(8,128)S(1)} %copy-done.8, f32[512,512]{1,0:T(8,128)S(1)} %convolution_select_fusion), kind=kOutput, calls=%fused_computation.33 | convolution fusion | flops 805830400 | bytes 3671040 | tf_op jit(solution)/shard_map/dot_general | solution.py:59
  116.0 0.0 copy-done.4
  116.0 0.6 multiply_reduce_fusion.1
  116.6 7.3 %psum.31 = f32[]{:T(128)} all-reduce(f32[]{:T(128)} %get-tuple-element.12), channel_id=1, replica_groups=mesh['ga'=8,'band'=4] {'band'}, use_global_device_ids=true, to_apply=%region_11.12 | all-reduce | flops 1 | bytes 8 | tf_op jit(solution)/shard_map/psum | solution.py:100
  123.9 4.6 %fusion.47 = f32[1024,256]{1,0:T(8,128)S(1)} fusion(f32[512,1024]{1,0:T(8,128)S(1)} %convolution_multiply_fusion, f32[512,256]{1,0:T(8,128)} %get-tuple-element.20), kind=kOutput, calls=%fused_computation.80 | convolution fusion | flops 1610612736 | bytes 3670016 | tf_op jit(solution)/shard_map/dot_general | solution.py:95
  128.6 0.0 copy-done.5
  128.6 0.0 copy-done.1
  128.6 0.0 copy-start.3
  128.6 5.1 %fusion.1 = f32[1,1024,256]{2,1,0:T(8,128)S(1)} fusion(f32[1024,256]{1,0:T(8,128)S(1)} %fusion.47, f32[512,1024]{1,0:T(8,128)S(1)} %copy-done.1, f32[512,256]{1,0:T(8,128)S(1)} %copy-done.5, f32[2,1024,256]{2,1,0:T(8,128)} %param.8, f32[256]{0:T(256)S(1)} %get-tuple-element.13, f32[1024]{0:T(1024)S(1)} %add_multiply_fusion.3), kind=kOutput, calls=%fused_computation.8 | convolution fusion | flops 1611661312 | bytes 5772288 | tf_op jit(solution)/shard_map/dot_general | solution.py:97
  133.7 0.0 copy-done.10
  133.7 0.0 copy-done.3
  133.7 0.0 copy-done.6
  133.7 0.0 copy-done.7
  133.7 3.8 %fusion.3 = f32[1,1024,256]{2,1,0:T(8,128)S(1)} fusion(f32[1024,256]{1,0:T(8,128)S(1)} %copy-done.7, f32[512,1024]{1,0:T(8,128)S(1)} %copy-done.1, f32[512,256]{1,0:T(8,128)S(1)} %copy-done.6, f32[2,1024,256]{2,1,0:T(8,128)S(1)} %copy-done.3, f32[256]{0:T(256)S(1)} %get-tuple-element.13, f32[1024]{0:T(1024)S(1)} %add_multiply_fusion.3), kind=kOutput, calls=%fused_computation.11 | convolution fusion | flops 1611661312 | bytes 5772288 | tf_op jit(solution)/shard_map/dot_general | solution.py:94
  137.5 1.5 pad_maximum_fusion
  (15 shorter events, 0.1 us)
Async XLA Ops:
  7.2 100.5 %all-reduce.3.cloned.1.call-start = ((), (), s32[]{:S(2)}) async-start(), calls=%async_computation | async-start | bytes 2097152 | tf_op jit(solution)/shard_map/psum | solution.py:87
  15.5 7.8 %copy-start = (f32[512,1024]{1,0:T(8,128)}, f32[512,1024]{1,0:T(8,128)S(1)}, u32[]{:S(2)}) copy-start(f32[512,1024]{1,0:T(8,128)S(1)} %multiply_negate_fusion) | copy-start | bytes 6291460
  15.5 2.4 %copy-start.2 = (f32[2,1024,256]{2,1,0:T(8,128)S(1)}, f32[2,1024,256]{2,1,0:T(8,128)}, u32[]{:S(2)}) copy-start(f32[2,1024,256]{2,1,0:T(8,128)} %param.8) | copy-start | bytes 6291460
  25.3 1.1 copy-start.9
  109.7 6.3 %copy-start.4 = (f32[512,256]{1,0:T(8,128)}, f32[512,256]{1,0:T(8,128)S(1)}, u32[]{:S(2)}) copy-start(f32[512,256]{1,0:T(8,128)S(1)} %fusion.17) | copy-start | bytes 1572868
  109.7 4.4 %copy-start.8 = (f32[2,512,256]{2,1,0:T(8,128)S(1)}, f32[2,512,256]{2,1,0:T(8,128)}, u32[]{:S(2)}) copy-start(f32[2,512,256]{2,1,0:T(8,128)} %all-reduce.3.cloned.1.call-done) | copy-start | bytes 3145732
  114.2 1.8 %copy-start.11 = (f32[256]{0:T(256)S(1)}, f32[256]{0:T(256)}, u32[]{:S(2)}) copy-start(f32[256]{0:T(256)} %param.15) | copy-start | bytes 3076
  116.0 12.6 %copy-start.5 = (f32[512,256]{1,0:T(8,128)S(1)}, f32[512,256]{1,0:T(8,128)}, u32[]{:S(2)}) copy-start(f32[512,256]{1,0:T(8,128)} %copy-done.4) | copy-start | bytes 1572868
  116.6 17.1 %copy-start.10 = (f32[256]{0:T(256)}, f32[256]{0:T(256)S(1)}, u32[]{:S(2)}) copy-start(f32[256]{0:T(256)S(1)} %get-tuple-element.13) | copy-start | bytes 3076
  123.9 4.7 %copy-start.1 = (f32[512,1024]{1,0:T(8,128)S(1)}, f32[512,1024]{1,0:T(8,128)}, u32[]{:S(2)}) copy-start(f32[512,1024]{1,0:T(8,128)} %copy-done) | copy-start | bytes 6291460
  128.6 5.1 %copy-start.3 = (f32[2,1024,256]{2,1,0:T(8,128)S(1)}, f32[2,1024,256]{2,1,0:T(8,128)}, u32[]{:S(2)}) copy-start(f32[2,1024,256]{2,1,0:T(8,128)} %param.8) | copy-start | bytes 6291460
  128.6 5.1 %copy-start.6 = (f32[512,256]{1,0:T(8,128)S(1)}, f32[512,256]{1,0:T(8,128)}, u32[]{:S(2)}) copy-start(f32[512,256]{1,0:T(8,128)} %get-tuple-element.20) | copy-start | bytes 1572868
  128.6 5.1 %copy-start.7 = (f32[1024,256]{1,0:T(8,128)S(1)}, f32[1024,256]{1,0:T(8,128)}, u32[]{:S(2)}) copy-start(f32[1024,256]{1,0:T(8,128)} %fusion.46) | copy-start | bytes 3145732
Sparse Core Ops, SparseCore 0:
  26.5 81.1 all-reduce.2
where the time goes:
time: 146 us
  waiting for transfers between devices  54.6 us (37%)
  matrix products  35.2 us (24%)
  blocking collectives  30.9 us (21%)
  between operations  14.3 us (10%)
  other arithmetic  7.34 us (5%)
  local copies, waits for them, and re-layouts  3.36 us (2%)
    psum x1, waiting for transfers between devices, on_device(): summed = lax.psum((proj_part, kin_part, norm_part), 'ga')  54.6 us
    psum x1, blocking collectives, on_device(): summed = lax.psum((proj_part, kin_part, norm_part), 'ga')  23.6 us
    psum x1, blocking collectives, on_device(): energy = lax.psum(jnp.sum(occupation * nonlocal_share), 'band')  7.33 us
    dot_general x1, matrix products, on_device(): lax.dot_general(beta_im, mixed_proj[0], contract, precision=HIGHEST_PRECI...  5.07 us
    dot_general x1, matrix products, on_device(): lax.dot_general(beta_re, mixed_proj[1], contract, precision=HIGHEST_PRECI...  4.64 us
    dot_general x1, matrix products, on_device(): lax.dot_general(beta_re, mixed_proj[0], contract, precision=HIGHEST_PRECI...  4.43 us
    dot_general x1, matrix products, on_device(): lax.dot_general(beta_im, mixed_proj[1], contract, precision=HIGHEST_PRECI...  3.76 us
  transfers between devices with their start and end apart: 1, of which 1 were waited for; matrix products, arithmetic and copies ran while one was open for 2% of the time, Pallas kernels for 0%

commit v1 on v0

v1 whole, which is shorter than its diff:
```python
import functools

import jax
import jax.numpy as jnp
from jax import lax
from jax.experimental import pallas as pl
from jax.experimental.pallas import tpu as pltpu
from jax.sharding import PartitionSpec as P

PROJ = 512
KINETIC_SCALE = 0.005
EPSILON = 1e-06
MESH = pl.DeviceIdType.MESH
F32 = jnp.float32
BF16 = jnp.bfloat16
TILE = 128
LANES = 128
COS = (1.0, -19.739208221435547, 64.93939208984375, -85.45665740966797, 60.24212646484375, -26.404630661010742, 7.800022125244141, -1.4529874324798584)
SIN = (6.2831854820251465, -41.34170150756836, 81.60513305664062, -76.7030029296875, 42.02585220336914, -14.899578094482422, 3.2377800941467285)


def split(x):
    high = x.astype(BF16)
    return high, (x - high.astype(F32)).astype(BF16)


def mm(a, b):
    return jnp.dot(a, b, preferred_element_type=F32)


def mm_t(a, b):
    return lax.dot_general(a, b, (((1,), (1,)), ((), ())), preferred_element_type=F32)


def poly(coefs, z):
    value = jnp.full_like(z, coefs[-1])
    for c in coefs[-2::-1]:
        value = value * z + c
    return value


def kernel(
    n_ga, n_band, kmax,
    waves, miller, positions, ff, coupling, species, sizes, occupation,
    residual, estimate, energy,
    beta, beta_t, psi_h, psi_l, ff_pad, cp_pad, ff_cat, cs_cat, owner_s, channel_s, crow_h, crow_l, dense_h, dense_l,
    part, landed, proj, mix_h, mix_l, stats, shares, kin_s,
    rs_send, rs_recv, ag_send, ag_recv, st_send, st_recv, en_send, en_recv,
):
    me = lax.axis_index("ga")
    my_band = lax.axis_index("band")
    rows = PROJ // n_ga
    n_blocks = PROJ // TILE
    per_block = TILE // rows
    nspec = ff.shape[0]
    kpad = -(-kmax // 8) * 8
    atoms = sizes.shape[1]
    local_g = miller.shape[1]
    bands = occupation.shape[1]

    barrier = pltpu.get_barrier_semaphore()

    def greet_ga(d, carry):
        pl.semaphore_signal(barrier, inc=1, device_id=(lax.rem(me + d, n_ga), my_band), device_id_type=MESH)
        return carry

    def greet_band(d, carry):
        pl.semaphore_signal(barrier, inc=1, device_id=(me, lax.rem(my_band + d, n_band)), device_id_type=MESH)
        return carry

    lax.fori_loop(1, n_ga, greet_ga, 0)
    lax.fori_loop(1, n_band, greet_band, 0)

    size_row = jnp.broadcast_to(sizes[...].astype(F32), (8, atoms))
    upper = (
        lax.broadcasted_iota(jnp.int32, (atoms, atoms), 0) <= lax.broadcasted_iota(jnp.int32, (atoms, atoms), 1)
    ).astype(F32).astype(BF16)
    ends = mm(size_row.astype(BF16), upper)[0:1]
    starts = ends - size_row[0:1]
    column = lax.broadcasted_iota(jnp.int32, (PROJ, atoms), 0).astype(F32)
    owner = jnp.where((column >= starts) & (column < ends), 1.0, 0.0).astype(F32)
    start_of = jnp.sum(owner * starts, axis=1, keepdims=True)
    species_of = jnp.sum(owner * species[...].astype(F32), axis=1, keepdims=True)
    channel = column[:, 0:1] - start_of
    row_index = species_of * float(kpad) + channel
    lane = lax.broadcasted_iota(jnp.int32, (PROJ, LANES), 1).astype(F32)
    row_hot = jnp.where(row_index == lane, 1.0, 0.0).astype(BF16)
    channel_s[...] = jnp.where(channel == lane, 1.0, 0.0).astype(BF16)
    blank = jnp.zeros((PROJ, LANES - atoms), BF16)
    owner_b = owner.astype(BF16)
    owner_s[:, 0:LANES] = row_hot
    owner_s[:, LANES:2 * LANES] = jnp.concatenate([owner_b, blank], axis=1)
    owner_s[:, 2 * LANES:3 * LANES] = jnp.concatenate([blank, owner_b], axis=1)

    ff_pad[...] = jnp.zeros_like(ff_pad)
    cp_pad[...] = jnp.zeros_like(cp_pad)
    for s in range(nspec):
        ff_pad[s * kpad:s * kpad + kmax, :] = ff[s]
        cp_pad[s * kpad:s * kpad + kmax, 0:kmax] = coupling[s]
    high, low = split(ff_pad[...])
    ff_cat[0:LANES] = high
    ff_cat[LANES:2 * LANES] = low

    miller_f = miller[...].astype(F32)
    turns = (
        positions[:, 0:1] * miller_f[0:1] + positions[:, 1:2] * miller_f[1:2] + positions[:, 2:3] * miller_f[2:3]
    )
    turns = turns - jnp.round(turns)
    square = turns * turns
    cosine = poly(COS, square)
    sine = turns * poly(SIN, square)
    for at, value in ((0, cosine), (LANES - atoms, sine)):
        high, low = split(value)
        cs_cat[at:at + atoms] = high
        cs_cat[LANES + at:LANES + at + atoms] = low

    for i in range(2):
        high, low = split(waves[i])
        psi_h[:, i * bands:(i + 1) * bands] = high
        psi_l[:, i * bands:(i + 1) * bands] = low

    pl.semaphore_wait(barrier, n_ga - 1 + n_band - 1)

    def rs_copy(target, source):
        return pltpu.make_async_remote_copy(
            src_ref=part.at[target], dst_ref=landed.at[source], send_sem=rs_send.at[target],
            recv_sem=rs_recv.at[source], device_id=(target, my_band), device_id_type=MESH,
        )

    my_block = me // per_block
    order = sorted(range(n_blocks), key=lambda d: -min(d, n_blocks - d))

    def project(step, carry):
        offset = order[0]
        for k in range(1, n_blocks):
            offset = jnp.where(step == k, order[k], offset)
        block = lax.rem(my_block + offset, n_blocks)
        at = pl.ds(pl.multiple_of(block * TILE, TILE), TILE)
        hot = owner_s[at, 0:LANES]
        radial = mm(jnp.concatenate([hot, hot], axis=1), ff_cat[...])
        hot = owner_s[at, LANES:2 * LANES]
        b_re = radial * mm(jnp.concatenate([hot, hot], axis=1), cs_cat[...])
        hot = owner_s[at, 2 * LANES:3 * LANES]
        b_im = -(radial * mm(jnp.concatenate([hot, hot], axis=1), cs_cat[...]))
        re_h, re_l = split(b_re)
        im_h, im_l = split(b_im)
        beta[0, at] = re_h
        beta[1, at] = im_h
        beta[2, at] = re_l
        beta[3, at] = im_l
        first = mm(jnp.concatenate([re_h, im_h, re_l, im_l], axis=0), psi_h[...])
        second = mm(jnp.concatenate([re_h, im_h], axis=0), psi_l[...])
        both = first[0:2 * TILE] + first[2 * TILE:] + second
        with_re = both[0:TILE]
        with_im = both[TILE:]
        p_re = with_re[:, 0:bands] + with_im[:, bands:]
        p_im = with_re[:, bands:] - with_im[:, 0:bands]
        for i in range(per_block):
            target = block * per_block + i
            part[target, :, 0:bands] = p_re[i * rows:(i + 1) * rows]
            part[target, :, bands:] = p_im[i * rows:(i + 1) * rows]
        for i in range(per_block):
            target = block * per_block + i

            @pl.when(target != me)
            def _():
                rs_copy(target, me).start()

        return carry

    lax.fori_loop(0, n_blocks, project, 0)

    kin_row = (
        0.5 * KINETIC_SCALE
        * (miller_f[0:1] * miller_f[0:1] + miller_f[1:2] * miller_f[1:2] + miller_f[2:3] * miller_f[2:3])
    )
    kin_s[...] = jnp.broadcast_to(kin_row, (LANES, local_g)).T
    for half in range(bands // LANES):
        lanes = pl.ds(half * LANES, LANES)
        re = waves[0, :, lanes]
        im = waves[1, :, lanes]
        density = re * re + im * im
        stats[me, 0:1, lanes] = jnp.sum(kin_s[...] * density, axis=0, keepdims=True)
        stats[me, 1:2, lanes] = jnp.sum(density, axis=0, keepdims=True)
    stats[me, 2:8] = jnp.zeros((6, bands), F32)

    def st_copy(target, source):
        return pltpu.make_async_remote_copy(
            src_ref=stats.at[source], dst_ref=stats.at[source], send_sem=st_send.at[target],
            recv_sem=st_recv.at[source], device_id=(target, my_band), device_id_type=MESH,
        )

    def each_ga(action):
        def body(d, carry):
            action(lax.rem(me + d, n_ga))
            return carry

        lax.fori_loop(1, n_ga, body, 0)

    each_ga(lambda peer: st_copy(peer, me).start())

    for k in range(4):
        def turn(block, carry):
            at = pl.ds(pl.multiple_of(block * TILE, TILE), TILE)
            to = pl.ds(pl.multiple_of((k % 2) * PROJ + block * TILE, TILE), TILE)
            beta_t[k // 2, :, to] = beta[k, at].astype(F32).T.astype(BF16)
            return carry

        lax.fori_loop(0, n_blocks, turn, 0)

    high, low = split(cp_pad[...])
    crow_h[...] = mm(owner_s[:, 0:LANES], high).astype(BF16)
    crow_l[...] = mm(owner_s[:, 0:LANES], low).astype(BF16)
    windows = [min(max(TILE * i - TILE // 2, 0), PROJ - 2 * TILE) for i in range(n_blocks)]
    for i in range(n_blocks):
        at = pl.ds(i * TILE, TILE)
        window = pl.ds(windows[i], 2 * TILE)
        same = mm_t(owner_s[at, LANES:2 * LANES], owner_s[window, LANES:2 * LANES])
        dense_h[at] = jnp.where(same > 0.5, mm_t(crow_h[at], channel_s[window]), 0.0).astype(BF16)
        dense_l[at] = jnp.where(same > 0.5, mm_t(crow_l[at], channel_s[window]), 0.0).astype(BF16)

    each_ga(lambda peer: rs_copy(me, peer).wait_recv())
    total = part[me]
    total = lax.fori_loop(1, n_ga, lambda d, t: t + landed[lax.rem(me + d, n_ga)], total)
    proj[me] = total

    def ag_copy(target, source):
        return pltpu.make_async_remote_copy(
            src_ref=proj.at[source], dst_ref=proj.at[source], send_sem=ag_send.at[target],
            recv_sem=ag_recv.at[source], device_id=(target, my_band), device_id_type=MESH,
        )

    each_ga(lambda peer: ag_copy(peer, me).start())
    each_ga(lambda peer: st_copy(me, peer).wait_recv())
    summed = stats[0]
    for s in range(1, n_ga):
        summed = summed + stats[s]
    kin_sum = summed[0:1]
    norm_sum = summed[1:2]
    each_ga(lambda peer: ag_copy(me, peer).wait_recv())

    gathered = proj[...].reshape(PROJ, 2 * bands)
    p_high, p_low = split(gathered)
    nonlocal_sum = jnp.zeros((1, bands), F32)
    for i in range(n_blocks):
        at = pl.ds(i * TILE, TILE)
        w = windows[i]
        near_h = p_high[w:w + 2 * TILE]
        near_l = p_low[w:w + 2 * TILE]
        mixed = mm(dense_h[at], near_h) + mm(dense_h[at], near_l) + mm(dense_l[at], near_h)
        product = jnp.sum(gathered[i * TILE:(i + 1) * TILE] * mixed, axis=0, keepdims=True)
        nonlocal_sum = nonlocal_sum + product[:, 0:bands] + product[:, bands:]
        below = pl.ds(PROJ + i * TILE, TILE)
        for ref, value in zip((mix_h, mix_l), split(mixed)):
            ref[at] = value
            ref[below, 0:bands] = -value[:, bands:]
            ref[below, bands:] = value[:, 0:bands]
    inverse = norm_sum + EPSILON
    quotient = (kin_sum + nonlocal_sum) / inverse
    estimate[...] = quotient
    share = jnp.sum(occupation[...] * nonlocal_sum / inverse)
    shares[my_band] = jnp.full((8, LANES), share, F32)

    def en_copy(target, source):
        return pltpu.make_async_remote_copy(
            src_ref=shares.at[source], dst_ref=shares.at[source], send_sem=en_send.at[target],
            recv_sem=en_recv.at[source], device_id=(me, target), device_id_type=MESH,
        )

    def each_band(action):
        def body(d, carry):
            action(lax.rem(my_band + d, n_band))
            return carry

        lax.fori_loop(1, n_band, body, 0)

    each_band(lambda peer: en_copy(peer, my_band).start())

    span = min(256, local_g)

    def apply(block, carry):
        at = pl.ds(pl.multiple_of(block * span, span), span)
        b_high = beta_t[0, at]
        applied = mm(b_high, mix_h[...]) + mm(beta_t[1, at], mix_h[...]) + mm(b_high, mix_l[...])
        kin = kin_s[at]
        shifted = jnp.concatenate([kin] * (bands // LANES), axis=1) - quotient
        residual[0, at] = shifted * waves[0, at] + applied[:, 0:bands]
        residual[1, at] = shifted * waves[1, at] + applied[:, bands:]
        return carry

    lax.fori_loop(0, local_g // span, apply, 0)

    each_band(lambda peer: en_copy(my_band, peer).wait_recv())
    whole = shares[0]
    for s in range(1, n_band):
        whole = whole + shares[s]
    energy[...] = whole
    each_ga(lambda peer: rs_copy(peer, me).wait_send())
    each_ga(lambda peer: st_copy(peer, me).wait_send())
    each_ga(lambda peer: ag_copy(peer, me).wait_send())
    each_band(lambda peer: en_copy(peer, my_band).wait_send())


def on_device(n_ga, n_band, waves, miller, positions, form_factors, coupling, species, block_sizes, occupation):
    nspec, kmax, local_g = form_factors.shape
    bands = waves.shape[2]
    atoms = block_sizes.shape[0]
    rows = PROJ // n_ga
    vmem = pl.BlockSpec(memory_space=pltpu.VMEM)
    dma = pltpu.SemaphoreType.DMA
    residual, estimate, energy = pl.pallas_call(
        functools.partial(kernel, n_ga, n_band, kmax),
        out_shape=(
            jax.ShapeDtypeStruct((2, local_g, bands), F32),
            jax.ShapeDtypeStruct((1, bands), F32),
            jax.ShapeDtypeStruct((8, LANES), F32),
        ),
        in_specs=[vmem] * 8,
        out_specs=(vmem, vmem, vmem),
        scratch_shapes=[
            pltpu.VMEM((4, PROJ, local_g), BF16),
            pltpu.VMEM((2, local_g, 2 * PROJ), BF16),
            pltpu.VMEM((local_g, 2 * bands), BF16),
            pltpu.VMEM((local_g, 2 * bands), BF16),
            pltpu.VMEM((LANES, local_g), F32),
            pltpu.VMEM((LANES, LANES), F32),
            pltpu.VMEM((2 * LANES, local_g), BF16),
            pltpu.VMEM((2 * LANES, local_g), BF16),
            pltpu.VMEM((PROJ, 3 * LANES), BF16),
            pltpu.VMEM((PROJ, LANES), BF16),
            pltpu.VMEM((PROJ, LANES), BF16),
            pltpu.VMEM((PROJ, LANES), BF16),
            pltpu.VMEM((PROJ, 2 * TILE), BF16),
            pltpu.VMEM((PROJ, 2 * TILE), BF16),
            pltpu.VMEM((n_ga, rows, 2 * bands), F32),
            pltpu.VMEM((n_ga, rows, 2 * bands), F32),
            pltpu.VMEM((n_ga, rows, 2 * bands), F32),
            pltpu.VMEM((2 * PROJ, 2 * bands), BF16),
            pltpu.VMEM((2 * PROJ, 2 * bands), BF16),
            pltpu.VMEM((n_ga, 8, bands), F32),
            pltpu.VMEM((n_band, 8, LANES), F32),
            pltpu.VMEM((local_g, LANES), F32),
            dma((n_ga,)), dma((n_ga,)), dma((n_ga,)), dma((n_ga,)),
            dma((n_ga,)), dma((n_ga,)), dma((n_band,)), dma((n_band,)),
        ],
        compiler_params=pltpu.CompilerParams(
            collective_id=0, has_side_effects=True, vmem_limit_bytes=48 * 1024 * 1024
        ),
    )(
        waves, miller, positions, form_factors, coupling,
        species.reshape(1, atoms), block_sizes.reshape(1, atoms), occupation.reshape(1, bands),
    )
    return residual, estimate.reshape(bands), energy[0, 0]


def solution(mesh):
    in_specs = (
        P(None, "ga", "band"),
        P(None, "ga"),
        P(),
        P(None, None, "ga"),
        P(),
        P(),
        P(),
        P("band"),
    )
    out_specs = (P(None, "ga", "band"), P("band"), P())
    body = functools.partial(on_device, mesh.shape["ga"], mesh.shape["band"])
    return jax.shard_map(body, mesh=mesh, in_specs=in_specs, out_specs=out_specs, check_vma=False)
```

time: 146 us -> 74.4 us (0.51)
  the two profiles are of different devices: /device:TPU:0 before, /device:TPU:31 now
where the time goes in v1:
time: 74.4 us; the launch traced here: 74 us
  Pallas kernels  64 us (86%)
  local copies, waits for them, and re-layouts  9.36 us (13%)
    pallas_call x1, Pallas kernels, on_device(): pl.pallas_call(functools.partial(kernel, n_ga, n_band, kmax), out_shape=(...  64 us
    unnamed x15, local copies, waits for them, and re-layouts  8.85 us

profile of v1, /device:TPU:31, one launch (start us, length us, event | category | flops | bytes accessed | tf_op | source)
XLA Modules:
  0.0 74.0 jit_solution(13108373118713610274)
XLA Ops:
  0.6 0.8 %copy.11.positions = f32[64,3]{1,0:T(8,128)S(1)} copy(f32[64,3]{0,1:T(4,128)} %param.10) | data formatting | bytes 1536 | tf_op args[2]
  1.4 0.8 %copy.13.coupling = f32[4,18,18]{2,1,0:T(8,128)S(1)} copy(f32[4,18,18]{2,0,1:T(4,128)} %param.12) | data formatting | bytes 10368 | tf_op args[4]
  2.2 1.1 %copy.12.ff = f32[4,18,1024]{2,1,0:T(8,128)S(1)} copy(f32[4,18,1024]{2,0,1:T(4,128)} %param.11) | data formatting | bytes 589824 | tf_op args[3]
  3.3 0.0 copy-start
  3.3 1.6 %copy-done = f32[2,1024,256]{2,1,0:T(8,128)S(1)} copy-done((f32[2,1024,256]{2,1,0:T(8,128)S(1)}, f32[2,1024,256]{2,1,0:T(8,128)}, u32[]{:S(2)}) %copy-start) | copy-done | bytes 2097176
  4.9 0.0 copy-start.1
  4.9 0.7 copy-done.1
  5.6 0.0 copy-start.2
  5.6 0.7 copy-done.2
  6.3 0.0 copy-start.3
  6.3 0.7 copy-done.3
  7.0 0.0 copy-start.4
  7.0 0.7 copy-done.4
  7.6 64.0 %shard_map.103 = (f32[2,1024,256]{2,1,0:T(8,128)S(1)}, f32[1,256]{1,0:T(1,128)S(1)}, f32[8,128]{1,0:T(8,128)S(1)}) custom-call(f32[2,1024,256]{2,1,0:T(8,128)S(1)} %copy-done, s32[3,1024]{1,0:T(4,128)S(1)} %copy-done.1, f32[64,3]{1,0:T(8,128)S(1)} %copy.11.positions, f32[4,18,1024]{2,1,0:T(8,128)S(1)} %copy.12.ff, f32[4,18,18]{2,1,0:T(8,128)S(1)} %copy.13.coupling, ...), custom_call_target="tpu_custom_call" | custom-call | tf_op jit(solution)/shard_map/pallas_call | solution.py:311
  71.6 0.5 slice.3
  72.1 1.3 %copy.16 = f32[2,1024,256]{2,1,0:T(8,128)} copy(f32[2,1024,256]{2,1,0:T(8,128)S(1)} %get-tuple-element.12) | data formatting | bytes 4194304
  73.5 0.6 copy.17
Async XLA Ops:
  3.3 1.6 %copy-start = (f32[2,1024,256]{2,1,0:T(8,128)S(1)}, f32[2,1024,256]{2,1,0:T(8,128)}, u32[]{:S(2)}) copy-start(f32[2,1024,256]{2,1,0:T(8,128)} %waves.1) | copy-start | bytes 6291460
  4.9 0.7 copy-start.1
  5.6 0.7 copy-start.2
  6.3 0.7 copy-start.3
  7.0 0.7 copy-start.4

commit v2 on v1

v2 whole, which is shorter than its diff:
```python
import functools

import jax
import jax.numpy as jnp
from jax import lax
from jax.experimental import pallas as pl
from jax.experimental.pallas import tpu as pltpu
from jax.sharding import PartitionSpec as P

PROJ = 512
KINETIC_SCALE = 0.005
EPSILON = 1e-06
MESH = pl.DeviceIdType.MESH
F32 = jnp.float32
BF16 = jnp.bfloat16
TILE = 128
LANES = 128
COS = (1.0, -19.739208221435547, 64.93939208984375, -85.45665740966797, 60.24212646484375, -26.404630661010742, 7.800022125244141, -1.4529874324798584)
SIN = (6.2831854820251465, -41.34170150756836, 81.60513305664062, -76.7030029296875, 42.02585220336914, -14.899578094482422, 3.2377800941467285)


def split(x):
    high = x.astype(BF16)
    return high, (x - high.astype(F32)).astype(BF16)


def mm(a, b):
    return jnp.dot(a, b, preferred_element_type=F32)


def mm_t(a, b):
    return lax.dot_general(a, b, (((1,), (1,)), ((), ())), preferred_element_type=F32)


def poly(coefs, z):
    value = jnp.full_like(z, coefs[-1])
    for c in coefs[-2::-1]:
        value = value * z + c
    return value


def kernel(
    n_ga, n_band, kmax,
    waves_in, miller_in, positions_in, ff_in, coupling_in, species_in, sizes_in, occupation_in,
    residual, estimate, energy,
    waves, miller, positions, ff, coupling, species, sizes, occupation,
    beta, beta_t, psi_h, psi_l, ff_pad, cp_pad, pos_pad, ff_cat, cs_cat, owner_s, channel_s, crow_h, crow_l, dense_h, dense_l,
    part, paired, landed, proj, mix_h, mix_l, stats, shares, kin_s,
    in_sems, pair_send, pair_recv, line_send, line_recv, ag_send, ag_recv, fw_send, st_send, st_recv, en_send, en_recv,
):
    me = lax.axis_index("ga")
    my_band = lax.axis_index("band")
    rows = PROJ // n_ga
    n_blocks = PROJ // TILE
    per_block = TILE // rows
    n_lines = n_ga // 2
    parity = lax.rem(me, 2)
    line = me // 2
    partner = line * 2 + 1 - parity
    nspec = ff.shape[1]
    atoms = sizes.shape[1]
    local_g = miller.shape[1]
    bands = occupation.shape[1]
    halves = bands // LANES
    wide = 2 * LANES

    loads = [
        pltpu.make_async_copy(source, target, in_sems.at[i])
        for i, (source, target) in enumerate((
            (sizes_in, sizes), (species_in, species), (positions_in, positions), (miller_in, miller),
            (ff_in, ff), (waves_in, waves), (coupling_in, coupling), (occupation_in, occupation),
        ))
    ]
    for load in loads:
        load.start()
    barrier = pltpu.get_barrier_semaphore()

    def greet_ga(d, carry):
        pl.semaphore_signal(barrier, inc=1, device_id=(lax.rem(me + d, n_ga), my_band), device_id_type=MESH)
        return carry

    def greet_band(d, carry):
        pl.semaphore_signal(barrier, inc=1, device_id=(me, lax.rem(my_band + d, n_band)), device_id_type=MESH)
        return carry

    lax.fori_loop(1, n_ga, greet_ga, 0)
    lax.fori_loop(1, n_band, greet_band, 0)

    ff_pad[...] = jnp.zeros_like(ff_pad)
    cp_pad[...] = jnp.zeros_like(cp_pad)
    pos_pad[...] = jnp.zeros_like(pos_pad)
    for load in loads[0:2]:
        load.wait()
    size_row = jnp.broadcast_to(sizes[...].astype(F32), (8, atoms))
    upper = (
        lax.broadcasted_iota(jnp.int32, (atoms, atoms), 0) <= lax.broadcasted_iota(jnp.int32, (atoms, atoms), 1)
    ).astype(F32).astype(BF16)
    ends = mm(size_row.astype(BF16), upper)[0:1]
    starts = ends - size_row[0:1]
    column = lax.broadcasted_iota(jnp.int32, (PROJ, atoms), 0).astype(F32)
    owner = jnp.where((column >= starts) & (column < ends), 1.0, 0.0).astype(F32)
    start_of = jnp.sum(owner * starts, axis=1, keepdims=True)
    species_of = jnp.sum(owner * species[...].astype(F32), axis=1, keepdims=True)
    channel = column[:, 0:1] - start_of
    row_index = channel * float(nspec) + species_of
    lane = lax.broadcasted_iota(jnp.int32, (PROJ, LANES), 1).astype(F32)
    row_hot = jnp.where(row_index == lane, 1.0, 0.0).astype(BF16)
    channel_s[...] = jnp.where(channel == lane, 1.0, 0.0).astype(BF16)
    blank = jnp.zeros((PROJ, LANES - atoms), BF16)
    owner_b = owner.astype(BF16)
    owner_s[:, 0:LANES] = row_hot
    owner_s[:, LANES:2 * LANES] = jnp.concatenate([owner_b, blank], axis=1)
    owner_s[:, 2 * LANES:3 * LANES] = jnp.concatenate([blank, owner_b], axis=1)

    for load in loads[2:4]:
        load.wait()
    pos_pad[0:3, 0:atoms] = positions[...]
    place = pos_pad[...].T[0:atoms]
    miller_f = miller[...].astype(F32)
    turns = place[:, 0:1] * miller_f[0:1] + place[:, 1:2] * miller_f[1:2] + place[:, 2:3] * miller_f[2:3]
    turns = turns - jnp.round(turns)
    square = turns * turns
    cosine = poly(COS, square)
    sine = turns * poly(SIN, square)
    for at, value in ((0, cosine), (LANES - atoms, sine)):
        high, low = split(value)
        cs_cat[at:at + atoms] = high
        cs_cat[LANES + at:LANES + at + atoms] = low

    loads[4].wait()
    for k in range(kmax):
        ff_pad[k * nspec:(k + 1) * nspec, :] = ff[k]
    high, low = split(ff_pad[...])
    ff_cat[0:LANES] = high
    ff_cat[LANES:2 * LANES] = low

    for load in loads[5:8]:
        load.wait()
    for i in range(2):
        high, low = split(waves[i])
        for h in range(halves):
            to = h * wide + i * LANES
            psi_h[:, to:to + LANES] = high[:, h * LANES:(h + 1) * LANES]
            psi_l[:, to:to + LANES] = low[:, h * LANES:(h + 1) * LANES]

    pl.semaphore_wait(barrier, n_ga - 1 + n_band - 1)

    def pair_copy(to_line):
        return pltpu.make_async_remote_copy(
            src_ref=part.at[to_line * 2 + 1 - parity], dst_ref=paired.at[to_line], send_sem=pair_send.at[to_line],
            recv_sem=pair_recv.at[to_line], device_id=(partner, my_band), device_id_type=MESH,
        )

    def line_copy(to_line, from_line):
        return pltpu.make_async_remote_copy(
            src_ref=part.at[to_line * 2 + parity], dst_ref=landed.at[from_line], send_sem=line_send.at[to_line],
            recv_sem=line_recv.at[from_line], device_id=(to_line * 2 + parity, my_band), device_id_type=MESH,
        )

    my_block = me // per_block
    lines_per_block = per_block // 2

    def block_of(step):
        rank = n_blocks - 1 - step
        swapped = 0
        bit = 1
        while bit < n_blocks:
            swapped = swapped + bit * lax.rem(lax.rem(my_block // bit, 2) + lax.rem(rank // bit, 2), 2)
            bit *= 2
        return swapped

    def pass_on(step):
        block = block_of(step)
        for i in range(lines_per_block):
            to_line = block * lines_per_block + i
            pair_copy(to_line).wait_recv()
            mine = part[to_line * 2 + parity] + paired[to_line]

            @pl.when(to_line == line)
            def _():
                landed[line] = mine

            @pl.when(to_line != line)
            def _():
                part[to_line * 2 + parity] = mine
                line_copy(to_line, line).start()

    def project(step, carry):
        block = block_of(step)
        at = pl.ds(pl.multiple_of(block * TILE, TILE), TILE)
        hot = owner_s[at, 0:LANES]
        radial = mm(jnp.concatenate([hot, hot], axis=1), ff_cat[...])
        hot = owner_s[at, LANES:2 * LANES]
        b_re = radial * mm(jnp.concatenate([hot, hot], axis=1), cs_cat[...])
        hot = owner_s[at, 2 * LANES:3 * LANES]
        b_im = -(radial * mm(jnp.concatenate([hot, hot], axis=1), cs_cat[...]))
        re_h, re_l = split(b_re)
        im_h, im_l = split(b_im)
        beta[0, at] = re_h
        beta[1, at] = im_h
        beta[2, at] = re_l
        beta[3, at] = im_l
        first = mm(jnp.concatenate([re_h, im_h, re_l, im_l], axis=0), psi_h[...])
        second = mm(jnp.concatenate([re_h, im_h], axis=0), psi_l[...])
        both = first[0:2 * TILE] + first[2 * TILE:] + second
        with_re = both[0:TILE]
        with_im = both[TILE:]
        for h in range(halves):
            a = h * wide
            b = a + LANES
            c = b + LANES
            p_re = with_re[:, a:b] + with_im[:, b:c]
            p_im = with_re[:, b:c] - with_im[:, a:b]
            for i in range(per_block):
                target = block * per_block + i
                part[target, h, :, 0:LANES] = p_re[i * rows:(i + 1) * rows]
                part[target, h, :, LANES:] = p_im[i * rows:(i + 1) * rows]
        for i in range(lines_per_block):
            pair_copy(block * lines_per_block + i).start()

        @pl.when(step > 0)
        def _():
            pass_on(step - 1)

        return carry

    lax.fori_loop(0, n_blocks, project, 0)

    kin_row = (
        0.5 * KINETIC_SCALE
        * (miller_f[0:1] * miller_f[0:1] + miller_f[1:2] * miller_f[1:2] + miller_f[2:3] * miller_f[2:3])
    )
    kin_s[...] = jnp.broadcast_to(kin_row, (LANES, local_g)).T
    for half in range(halves):
        lanes = pl.ds(half * LANES, LANES)
        re = waves[0, :, lanes]
        im = waves[1, :, lanes]
        density = re * re + im * im
        stats[me, 0:1, lanes] = jnp.sum(kin_s[...] * density, axis=0, keepdims=True)
        stats[me, 1:2, lanes] = jnp.sum(density, axis=0, keepdims=True)
    stats[me, 2:8] = jnp.zeros((6, bands), F32)

    def st_copy(target, source):
        return pltpu.make_async_remote_copy(
            src_ref=stats.at[source], dst_ref=stats.at[source], send_sem=st_send.at[target],
            recv_sem=st_recv.at[source], device_id=(target, my_band), device_id_type=MESH,
        )

    def each_ga(action):
        def body(d, carry):
            action(lax.rem(me + d, n_ga))
            return carry

        lax.fori_loop(1, n_ga, body, 0)

    each_ga(lambda peer: st_copy(peer, me).start())
    pass_on(n_blocks - 1)

    for k in range(4):
        def turn(block, carry):
            at = pl.ds(pl.multiple_of(block * TILE, TILE), TILE)
            to = pl.ds(pl.multiple_of((k % 2) * PROJ + block * TILE, TILE), TILE)
            beta_t[k // 2, :, to] = beta[k, at].astype(F32).T.astype(BF16)
            return carry

        lax.fori_loop(0, n_blocks, turn, 0)

    for k in range(kmax):
        cp_pad[k * nspec:(k + 1) * nspec, 0:kmax] = coupling[k]
    high, low = split(cp_pad[...])
    crow_h[...] = mm(owner_s[:, 0:LANES], high).astype(BF16)
    crow_l[...] = mm(owner_s[:, 0:LANES], low).astype(BF16)
    windows = [min(max(TILE * i - TILE // 2, 0), PROJ - 2 * TILE) for i in range(n_blocks)]
    for i in range(n_blocks):
        at = pl.ds(i * TILE, TILE)
        window = pl.ds(windows[i], 2 * TILE)
        same = mm_t(owner_s[at, LANES:2 * LANES], owner_s[window, LANES:2 * LANES])
        dense_h[at] = jnp.where(same > 0.5, mm_t(crow_h[at], channel_s[window]), 0.0).astype(BF16)
        dense_l[at] = jnp.where(same > 0.5, mm_t(crow_l[at], channel_s[window]), 0.0).astype(BF16)

    def each_line(action):
        def body(d, carry):
            action(lax.rem(line + d, n_lines))
            return carry

        lax.fori_loop(1, n_lines, body, 0)

    each_line(lambda other: line_copy(line, other).wait_recv())
    total = lax.fori_loop(1, n_lines, lambda d, t: t + landed[lax.rem(line + d, n_lines)], landed[line])
    for h in range(halves):
        proj[h, me] = total[h]

    def ag_copy(h, to_line, source):
        return pltpu.make_async_remote_copy(
            src_ref=proj.at[h, source], dst_ref=proj.at[h, source], send_sem=ag_send.at[h, to_line],
            recv_sem=ag_recv.at[h, source], device_id=(to_line * 2 + parity, my_band), device_id_type=MESH,
        )

    def fw_copy(h, source):
        return pltpu.make_async_remote_copy(
            src_ref=proj.at[h, source], dst_ref=proj.at[h, source], send_sem=fw_send.at[h, source // 2],
            recv_sem=ag_recv.at[h, source], device_id=(partner, my_band), device_id_type=MESH,
        )

    for h in range(halves):
        fw_copy(h, me).start()

        def send(other, h=h):
            ag_copy(h, other, me).start()

        each_line(send)

    def relay(h, d):
        source = lax.rem(line + d, n_lines) * 2 + parity
        ag_copy(h, line, source).wait_recv()
        fw_copy(h, source).start()

    def relay_first(d, carry):
        relay(0, d)
        return carry

    lax.fori_loop(1, n_lines, relay_first, 0)
    each_ga(lambda peer: st_copy(me, peer).wait_recv())
    summed = stats[0]
    for s in range(1, n_ga):
        summed = summed + stats[s]
    kin_sum = summed[0:1]
    norm_sum = summed[1:2]
    def en_copy(target, source):
        return pltpu.make_async_remote_copy(
            src_ref=shares.at[source], dst_ref=shares.at[source], send_sem=en_send.at[target],
            recv_sem=en_recv.at[source], device_id=(me, target), device_id_type=MESH,
        )

    def each_band(action):
        def body(d, carry):
            action(lax.rem(my_band + d, n_band))
            return carry

        lax.fori_loop(1, n_band, body, 0)

    inverse = norm_sum + EPSILON
    span = min(256, local_g)
    spans = local_g // span
    per_span = -(-(n_lines - 1) // spans)
    share = jnp.zeros((), F32)
    for h in range(halves):
        def arrive(d, carry, h=h):
            source = lax.rem(line + d, n_lines) * 2 + 1 - parity
            fw_copy(h, source).wait_recv()
            return carry

        lax.fori_loop(0, n_lines, arrive, 0)

        gathered = proj[h].reshape(PROJ, wide)
        p_high, p_low = split(gathered)
        nonlocal_sum = jnp.zeros((1, LANES), F32)
        for i in range(n_blocks):
            at = pl.ds(i * TILE, TILE)
            w = windows[i]
            near_h = p_high[w:w + 2 * TILE]
            near_l = p_low[w:w + 2 * TILE]
            mixed = mm(dense_h[at], near_h) + mm(dense_h[at], near_l) + mm(dense_l[at], near_h)
            product = jnp.sum(gathered[i * TILE:(i + 1) * TILE] * mixed, axis=0, keepdims=True)
            nonlocal_sum = nonlocal_sum + product[:, 0:LANES] + product[:, LANES:]
            below = pl.ds(PROJ + i * TILE, TILE)
            for ref, value in zip((mix_h, mix_l), split(mixed)):
                ref[at] = value
                ref[below, 0:LANES] = -value[:, LANES:]
                ref[below, LANES:] = value[:, 0:LANES]
        lanes = pl.ds(h * LANES, LANES)
        here = slice(h * LANES, (h + 1) * LANES)
        quotient = (kin_sum[:, here] + nonlocal_sum) / inverse[:, here]
        estimate[:, lanes] = quotient
        share = share + jnp.sum(occupation[:, lanes] * nonlocal_sum / inverse[:, here])
        if h == halves - 1:
            shares[my_band] = jnp.full((8, LANES), share, F32)
            each_band(lambda peer: en_copy(peer, my_band).start())

        def apply(block, carry, h=h, lanes=lanes, quotient=quotient):
            at = pl.ds(pl.multiple_of(block * span, span), span)
            b_high = beta_t[0, at]
            applied = mm(b_high, mix_h[...]) + mm(beta_t[1, at], mix_h[...]) + mm(b_high, mix_l[...])
            shifted = kin_s[at] - quotient
            residual[0, at, lanes] = shifted * waves[0, at, lanes] + applied[:, 0:LANES]
            residual[1, at, lanes] = shifted * waves[1, at, lanes] + applied[:, LANES:]
            if h + 1 < halves:
                for k in range(per_span):
                    d = block * per_span + k + 1

                    @pl.when(d < n_lines)
                    def _():
                        relay(h + 1, d)

            return carry

        lax.fori_loop(0, spans, apply, 0)

    each_band(lambda peer: en_copy(my_band, peer).wait_recv())
    whole = shares[0]
    for s in range(1, n_band):
        whole = whole + shares[s]
    energy[...] = whole
    def pair_done(to_line, carry):
        pair_copy(to_line).wait_send()
        return carry

    lax.fori_loop(0, n_lines, pair_done, 0)
    each_line(lambda other: line_copy(other, line).wait_send())
    for h in range(halves):
        def sent(other, h=h):
            ag_copy(h, other, me).wait_send()

        def relayed(d, carry, h=h):
            fw_copy(h, lax.rem(line + d, n_lines) * 2 + parity).wait_send()
            return carry

        each_line(sent)
        lax.fori_loop(0, n_lines, relayed, 0)
    each_ga(lambda peer: st_copy(peer, me).wait_send())
    each_band(lambda peer: en_copy(peer, my_band).wait_send())


def on_device(n_ga, n_band, waves, miller, positions, form_factors, coupling, species, block_sizes, occupation):
    nspec, kmax, local_g = form_factors.shape
    bands = waves.shape[2]
    atoms = block_sizes.shape[0]
    rows = PROJ // n_ga
    halves = bands // LANES
    vmem = pl.BlockSpec(memory_space=pltpu.VMEM)
    hbm = pl.BlockSpec(memory_space=pltpu.HBM)
    dma = pltpu.SemaphoreType.DMA
    residual, estimate, energy = pl.pallas_call(
        functools.partial(kernel, n_ga, n_band, kmax),
        out_shape=(
            jax.ShapeDtypeStruct((2, local_g, bands), F32),
            jax.ShapeDtypeStruct((1, bands), F32),
            jax.ShapeDtypeStruct((8, LANES), F32),
        ),
        in_specs=[hbm] * 8,
        out_specs=(vmem, vmem, vmem),
        scratch_shapes=[
            pltpu.VMEM((2, local_g, bands), F32),
            pltpu.VMEM((3, local_g), jnp.int32),
            pltpu.VMEM((3, atoms), F32),
            pltpu.VMEM((kmax, nspec, local_g), F32),
            pltpu.VMEM((kmax, nspec, kmax), F32),
            pltpu.VMEM((1, atoms), jnp.int32),
            pltpu.VMEM((1, atoms), jnp.int32),
            pltpu.VMEM((1, bands), F32),
            pltpu.VMEM((4, PROJ, local_g), BF16),
            pltpu.VMEM((2, local_g, 2 * PROJ), BF16),
            pltpu.VMEM((local_g, 2 * bands), BF16),
            pltpu.VMEM((local_g, 2 * bands), BF16),
            pltpu.VMEM((LANES, local_g), F32),
            pltpu.VMEM((LANES, LANES), F32),
            pltpu.VMEM((LANES, LANES), F32),
            pltpu.VMEM((2 * LANES, local_g), BF16),
            pltpu.VMEM((2 * LANES, local_g), BF16),
            pltpu.VMEM((PROJ, 3 * LANES), BF16),
            pltpu.VMEM((PROJ, LANES), BF16),
            pltpu.VMEM((PROJ, LANES), BF16),
            pltpu.VMEM((PROJ, LANES), BF16),
            pltpu.VMEM((PROJ, 2 * TILE), BF16),
            pltpu.VMEM((PROJ, 2 * TILE), BF16),
            pltpu.VMEM((n_ga, halves, rows, 2 * LANES), F32),
            pltpu.VMEM((n_ga // 2, halves, rows, 2 * LANES), F32),
            pltpu.VMEM((n_ga // 2, halves, rows, 2 * LANES), F32),
            pltpu.VMEM((halves, n_ga, rows, 2 * LANES), F32),
            pltpu.VMEM((2 * PROJ, 2 * LANES), BF16),
            pltpu.VMEM((2 * PROJ, 2 * LANES), BF16),
            pltpu.VMEM((n_ga, 8, bands), F32),
            pltpu.VMEM((n_band, 8, LANES), F32),
            pltpu.VMEM((local_g, LANES), F32),
            dma((8,)), dma((n_ga // 2,)), dma((n_ga // 2,)), dma((n_ga // 2,)), dma((n_ga // 2,)),
            dma((halves, n_ga // 2)), dma((halves, n_ga)), dma((halves, n_ga // 2)),
            dma((n_ga,)), dma((n_ga,)), dma((n_band,)), dma((n_band,)),
        ],
        compiler_params=pltpu.CompilerParams(
            collective_id=0, has_side_effects=True, vmem_limit_bytes=67_043_328
        ),
    )(
        waves, miller, positions.T, jnp.transpose(form_factors, (1, 0, 2)), jnp.transpose(coupling, (1, 0, 2)),
        species.reshape(1, atoms), block_sizes.reshape(1, atoms), occupation.reshape(1, bands),
    )
    return residual, estimate.reshape(bands), energy[0, 0]


def solution(mesh):
    in_specs = (
        P(None, "ga", "band"),
        P(None, "ga"),
        P(),
        P(None, None, "ga"),
        P(),
        P(),
        P(),
        P("band"),
    )
    out_specs = (P(None, "ga", "band"), P("band"), P())
    body = functools.partial(on_device, mesh.shape["ga"], mesh.shape["band"])
    return jax.shard_map(body, mesh=mesh, in_specs=in_specs, out_specs=out_specs, check_vma=False)
```

time: 74.4 us -> 56.4 us (0.76)
  the two profiles are of different devices: /device:TPU:31 before, /device:TPU:0 now
where the time goes in v2:
time: 56.4 us; the launch traced here: 56.1 us
  Pallas kernels  50.6 us (90%)
  local copies, waits for them, and re-layouts  4.81 us (9%)
  between operations  0.64 us (1%)
    pallas_call x1, Pallas kernels, on_device(): pl.pallas_call(functools.partial(kernel, n_ga, n_band, kmax), out_shape=(...  50.6 us
    unnamed x4, local copies, waits for them, and re-layouts  3.61 us
    slice x1, local copies, waits for them, and re-layouts, on_device(): return (residual, estimate.reshape(bands), energy[0, 0])  1.19 us

profile of v2, /device:TPU:0, one launch (start us, length us, event | category | flops | bytes accessed | tf_op | source)
XLA Modules:
  0.0 56.1 jit_solution(13910193831046146573)
XLA Ops:
  0.6 50.6 %shard_map.103 = (f32[2,1024,256]{2,1,0:T(8,128)}, f32[1,256]{1,0:T(1,128)}, f32[8,128]{1,0:T(8,128)}) custom-call(f32[2,1024,256]{2,1,0:T(8,128)} %waves_in.1, s32[3,1024]{1,0:T(4,128)} %miller_in.1, f32[3,64]{1,0:T(4,128)} %bitcast.10, f32[18,4,1024]{2,1,0:T(4,128)} %bitcast.8, f32[18,4,18]{2,1,0:T(4,128)} %bitcast.9, s32[1,64]{1,0:T(1,128)} %bitcast.13, ...), custom_call_target="tpu_custom_call" | custom-call | tf_op jit(solution)/shard_map/pallas_call | solution.py:433
  51.3 1.2 %slice.3 = f32[1,1]{1,0:T(1,128)} slice(f32[8,128]{1,0:T(8,128)} %get-tuple-element.8), slice={[0:1], [0:1]} | slice | bytes 8 | tf_op jit(solution)/shard_map/slice | solution.py:486
  52.5 0.0 copy-start
  52.5 3.0 %copy.13 = f32[2,1024,256]{2,1,0:T(8,128)} copy(f32[2,1024,256]{2,1,0:T(8,128)} %get-tuple-element.12) | data formatting | bytes 4194304
  55.5 0.0 copy-done
  55.5 0.6 %copy.14 = f32[256]{0:T(256)} copy(f32[256]{0:T(256)S(1)} %bitcast.12) | data formatting | bytes 2048
Async XLA Ops:
  52.5 3.0 %copy-start = (f32[1,256]{1,0:T(1,128)S(1)}, f32[1,256]{1,0:T(1,128)}, u32[]{:S(2)}) copy-start(f32[1,256]{1,0:T(1,128)} %get-tuple-element.7) | copy-start | bytes 3076

commit v3 on v2

--- a/solution.py
+++ b/solution.py
@@ -311,7 +311,7 @@
         each_line(send)
 
     def relay(h, d):
-        source = lax.rem(line + d, n_lines) * 2 + parity
+        source = lax.rem(line + n_lines - d, n_lines) * 2 + parity
         ag_copy(h, line, source).wait_recv()
         fw_copy(h, source).start()
 
@@ -400,7 +400,7 @@
     whole = shares[0]
     for s in range(1, n_band):
         whole = whole + shares[s]
-    energy[...] = whole
+    energy[...] = whole[0:1, 0:1]
     def pair_done(to_line, carry):
         pair_copy(to_line).wait_send()
         return carry
@@ -435,7 +435,7 @@
         out_shape=(
             jax.ShapeDtypeStruct((2, local_g, bands), F32),
             jax.ShapeDtypeStruct((1, bands), F32),
-            jax.ShapeDtypeStruct((8, LANES), F32),
+            jax.ShapeDtypeStruct((1, 1), F32),
         ),
         in_specs=[hbm] * 8,
         out_specs=(vmem, vmem, vmem),
@@ -483,7 +483,7 @@
         waves, miller, positions.T, jnp.transpose(form_factors, (1, 0, 2)), jnp.transpose(coupling, (1, 0, 2)),
         species.reshape(1, atoms), block_sizes.reshape(1, atoms), occupation.reshape(1, bands),
     )
-    return residual, estimate.reshape(bands), energy[0, 0]
+    return residual, estimate.reshape(bands), energy.reshape(())
 
 
 def solution(mesh):

time: 56.4 us -> 56.5 us (level)
  between operations: 0.64 us -> 2.33 us
  local copies, waits for them, and re-layouts: 4.81 us -> 3.61 us
    slice x1 -> x0, local copies, waits for them, and re-layouts: 1.19 us -> none  [on_device(): return (residual, estimate.reshape(bands), energy[0, 0])]
where the time goes in v3:
time: 56.5 us; the launch traced here: 56.3 us
  Pallas kernels  50.4 us (89%)
  local copies, waits for them, and re-layouts  3.61 us (6%)
  between operations  2.33 us (4%)
    pallas_call x1, Pallas kernels, on_device(): pl.pallas_call(functools.partial(kernel, n_ga, n_band, kmax), out_shape=(...  50.4 us
    unnamed x4, local copies, waits for them, and re-layouts  3.61 us

profile of v3, /device:TPU:0, one launch (start us, length us, event | category | flops | bytes accessed | tf_op | source)
XLA Modules:
  0.0 56.3 jit_solution(5516981425640691267)
XLA Ops:
  0.6 50.4 %shard_map.103 = (f32[2,1024,256]{2,1,0:T(8,128)}, f32[1,256]{1,0:T(1,128)}, f32[1,1]{1,0:T(1,128)}) custom-call(f32[2,1024,256]{2,1,0:T(8,128)} %waves_in.1, s32[3,1024]{1,0:T(4,128)} %miller_in.1, f32[3,64]{1,0:T(4,128)} %bitcast.10, f32[18,4,1024]{2,1,0:T(4,128)} %bitcast.8, f32[18,4,18]{2,1,0:T(4,128)} %bitcast.9, s32[1,64]{1,0:T(1,128)} %bitcast.13, ...), custom_call_target="tpu_custom_call" | custom-call | tf_op jit(solution)/shard_map/pallas_call | solution.py:433
  51.0 0.0 copy-start
  51.0 3.0 %copy.14 = f32[2,1024,256]{2,1,0:T(8,128)} copy(f32[2,1024,256]{2,1,0:T(8,128)} %get-tuple-element.12) | data formatting | bytes 4194304
  54.1 0.0 copy-done
  54.1 0.6 copy.15
Async XLA Ops:
  51.0 3.1 %copy-start = (f32[1,256]{1,0:T(1,128)S(1)}, f32[1,256]{1,0:T(1,128)}, u32[]{:S(2)}) copy-start(f32[1,256]{1,0:T(1,128)} %get-tuple-element.7) | copy-start | bytes 3076
